TPU v7x, 32 devices: a whole 2x2x4 slice. The times are simulated.
32 devices in a mesh: date: 16 (over z, y, x), pix: 2 (over core).
Axes of the slice: x: 2, y: 2, z: 4, core: 2. Of those that a mesh axis runs over, the one named last changes fastest.
Arguments:
- reflect: bfloat16 [64, 6, 16384], P('date', None, 'pix'), may hold values from -8 to 8
- cloud_free: int32 [64, 16384], P('date', 'pix'), may hold values from 0 to 1, as said below
- days: int32 [64], P('date'), may hold values from 1 to 2079, as said below
Outputs:
- median: float32 [6, 16384], P(None, 'pix')
- slope: float32 [6, 16384], P(None, 'pix')
Inputs may be any that keep to these rules, and one draw needn't show every extreme that they name: `cloud_free`: every pixel is clear on at least one of the first 32 dates and on at least one of the others; clear shares differ between tiles. `days`: strictly increasing.
All inputs are finite; a program needn't handle non-finite values.
Results may differ from a plain program's by a relative error of at most 0.0003.
Values may be sent and summed in bfloat16 or wider, within the bound.
A program may use at most 64 MiB of HBM per device.

v0:
```python
import jax
import jax.numpy as jnp
from jax import lax
from jax.sharding import PartitionSpec as P

ridge = 1.0
sentinel = 100.0


def count_ranks(carry, own, piece):

    def step(i, state):
        less, equal, count = state
        other = lax.dynamic_index_in_dim(piece, i, 0, keepdims=True).astype(jnp.float32)
        less = less + (other < own).astype(jnp.float32)
        equal = equal + (other == own).astype(jnp.float32)
        count = count + (other[0, 0] < 50.0).astype(jnp.float32)
        return (less, equal, count)

    return lax.fori_loop(0, piece.shape[0], step, carry)


def select_sums(values, valid, less, equal, count):
    lower = jnp.floor((count - 1.0) / 2.0)
    upper = jnp.floor(count / 2.0)
    low_pick = valid[:, None, :] * ((less <= lower) & (lower < less + equal)).astype(jnp.float32)
    high_pick = valid[:, None, :] * ((less <= upper) & (upper < less + equal)).astype(jnp.float32)
    return (
        jnp.sum(low_pick * values, 0),
        jnp.sum(low_pick, 0),
        jnp.sum(high_pick * values, 0),
        jnp.sum(high_pick, 0),
    )


def finish_median(low_num, low_den, high_num, high_den):
    return 0.5 * (low_num / jnp.maximum(low_den, 1.0) + high_num / jnp.maximum(high_den, 1.0))


def column_median(moved):
    column = moved.astype(jnp.float32)
    column_valid = (column[:, 0, :] < 50.0).astype(jnp.float32)
    zeros = jnp.zeros(column.shape, jnp.float32)
    start_carry = (zeros, zeros, jnp.zeros((column.shape[2],), jnp.float32))
    less, equal, count = count_ranks(start_carry, column, moved)
    low_num, low_den, high_num, high_den = select_sums(column, column_valid, less, equal, count)
    return (column, column_valid, finish_median(low_num, low_den, high_num, high_den))


def fit_slope(s_zero, s_one, s_two, s_y, s_ty):
    first = s_zero + ridge
    determinant = first * (s_two + ridge) - s_one * s_one
    return (first[None, :] * s_ty - s_one[None, :] * s_y) / determinant[None, :]


def local(reflect, cloud_free, days):
    values = reflect.astype(jnp.float32)
    valid = cloud_free.astype(jnp.float32)
    years = days.astype(jnp.float32) / 365.0
    csum = jnp.sum(values * valid[:, None, :], 2)
    cnt = jnp.sum(valid, 1)
    csum, cnt = lax.psum((csum, cnt), "pix")
    scene_mean = csum / jnp.maximum(cnt, 1.0)[:, None]
    marked = jnp.where(valid[:, None, :] > 0, values, sentinel).astype(jnp.bfloat16)
    shifted = values - scene_mean[:, :, None]
    weighted = valid[:, None, :] * shifted
    s_zero = jnp.sum(valid, 0)
    s_one = jnp.sum(years[:, None] * valid, 0)
    s_two = jnp.sum((years * years)[:, None] * valid, 0)
    s_y = jnp.sum(weighted, 0)
    s_ty = jnp.sum(years[:, None, None] * weighted, 0)
    moved = lax.all_to_all(marked, "date", split_axis=2, concat_axis=0, tiled=True)
    column, column_valid, part_median = column_median(moved)
    median = lax.all_gather(part_median, "date", axis=1, tiled=True)
    s_y, s_ty, s_zero, s_one, s_two = lax.psum((s_y, s_ty, s_zero, s_one, s_two), "date")
    slope = fit_slope(s_zero, s_one, s_two, s_y, s_ty)
    return (median, slope)


def solution(mesh):
    placed = (P("date", None, "pix"), P("date", "pix"), P("date"))
    return jax.shard_map(
        local,
        mesh=mesh,
        in_specs=placed,
        out_specs=(P(None, "pix"), P(None, "pix")),
        check_vma=False,
    )
```

profile of v0, /device:TPU:0, one launch (start us, length us, event | category | flops | bytes accessed | tf_op | source)
XLA Modules:
  0.0 414.7 jit_solution(17819752993265104546)
XLA Ops:
  7.9 1.8 convert_reduce_fusion.1
  9.7 0.9 convert_element_type.50
  10.7 1.0 broadcast_compare_fusion
  11.6 1.3 fusion.4
  12.9 2.6 all-reduce.2
  15.6 3.0 fusion.8
  18.6 8.5 %copy.37 = bf16[4,6,8192]{1,0,2:T(4,128)(2,1)} copy(bf16[4,6,8192]{2,0,1:T(4,128)(2,1)S(1)} %get-tuple-element.172) | data formatting | bytes 786432 | tf_op jit(solution)/shard_map/convert_element_type | solution.py:64
  27.2 14.3 %reshape.24 = bf16[16,2,6144]{2,1,0:T(2,128)(2,1)} reshape(bf16[8192,4,6]{2,1,0:T(4,128)(2,1)} %bitcast.17) | data formatting | bytes 786432
  41.5 8.2 %all-to-all-start = ((bf16[16,2,6144]{2,1,0:T(2,128)(2,1)}), bf16[16,2,6144]{2,1,0:T(2,128)(2,1)S(1)}, u32[]{:S(2)}, u32[]{:S(2)}) async-start(bf16[16,2,6144]{2,1,0:T(2,128)(2,1)} %reshape.24), calls=%async_computation | async-start | bytes 786432 | tf_op jit(solution)/shard_map/all_to_all | solution.py:72
  49.7 72.8 %all-reduce.6.cloned.1.call-done = (f32[8192]{0:T(1024)}, f32[8192]{0:T(1024)}, f32[8192]{0:T(1024)}) async-done(((f32[8192]{0:T(1024)}, f32[8192]{0:T(1024)}, f32[8192]{0:T(1024)}), (f32[8192]{0:T(1024)}, f32[8192]{0:T(1024)}, f32[8192]{0:T(1024)})) %all-reduce.6.cloned.1.call-update) | async-done | bytes 98320 | tf_op jit(solution)/shard_map/psum | solution.py:75
  122.5 0.8 broadcast_add_fusion
  123.4 114.3 %all-reduce.8.cloned.1.call-done = (f32[6,8192]{1,0:T(8,128)}, f32[6,8192]{1,0:T(8,128)}) async-done(((f32[6,8192]{1,0:T(8,128)}, f32[6,8192]{1,0:T(8,128)}), (f32[6,8192]{1,0:T(8,128)}, f32[6,8192]{1,0:T(8,128)})) %all-reduce.8.cloned.1.call-update) | async-done | bytes 393232 | tf_op jit(solution)/shard_map/psum | solution.py:75
  237.7 1.8 subtract_divide_fusion
  239.5 20.0 %reshape.25 = bf16[8192,4,6]{2,1,0:T(4,128)(2,1)} reshape(bf16[16,2,6144]{2,1,0:T(2,128)(2,1)S(1)} %all-to-all-done) | data formatting | bytes 786432
  259.5 12.9 %copy.38 = bf16[16,4,6,512]{3,2,1,0:T(8,128)(2,1)} copy(bf16[16,4,6,512]{2,1,3,0:T(4,128)(2,1)} %bitcast.18) | data formatting | bytes 786432 | tf_op jit(solution)/shard_map/all_to_all | solution.py:72
  272.3 1.2 bitcast_convert_fusion
  273.7 91.0 %while.18 = (s32[]{:T(128)}, f32[64,6,512]{2,1,0:T(8,128)S(1)}, f32[64,6,512]{2,1,0:T(8,128)S(1)}, f32[512]{0:T(512)S(1)}, bf16[64,6,512]{2,1,0:T(8,128)(2,1)}, ...) while((s32[]{:T(128)}, f32[64,6,512]{2,1,0:T(8,128)S(1)}, f32[64,6,512]{2,1,0:T(8,128)S(1)}, ...), condition=%wide.region_1.0_spmd.clone, body=%wide.region_0.0_spmd.clone.sunk | while | flops 1577987 | bytes 3985508 | solution.py:20
  273.7 0.7 dynamic-slice_convert_fusion.2
  275.1 0.7 dynamic-slice_convert_fusion.2
  276.5 0.7 dynamic-slice_convert_fusion.2
  277.9 0.7 dynamic-slice_convert_fusion.2
  279.4 0.7 dynamic-slice_convert_fusion.2
  280.8 0.7 dynamic-slice_convert_fusion.2
  282.2 0.7 dynamic-slice_convert_fusion.2
  283.6 0.7 dynamic-slice_convert_fusion.2
  285.1 0.7 dynamic-slice_convert_fusion.2
  286.5 0.7 dynamic-slice_convert_fusion.2
  292.2 0.7 dynamic-slice_convert_fusion.2
  293.6 0.7 dynamic-slice_convert_fusion.2
  295.0 0.7 dynamic-slice_convert_fusion.2
  365.1 1.6 fusion.1
  366.8 40.4 %all_gather.3 = f32[6,8192]{1,0:T(8,128)S(1)} all-gather(f32[6,512]{1,0:T(8,128)S(1)} %add_multiply_fusion), channel_id=1, replica_groups=mesh['date'=16,'pix'=2] {'date'}, dimensions={1}, use_global_device_ids=true | all-gather | bytes 208896 | tf_op jit(solution)/shard_map/all_gather | solution.py:74
  (260 shorter events, 82.1 us)
Async XLA Ops:
  7.2 115.4 %all-reduce.6.cloned.1.call-start = ((), (), s32[]{:S(2)}) async-start(), calls=%async_computation.1 | async-start | bytes 196608 | tf_op jit(solution)/shard_map/psum | solution.py:75
  9.7 228.0 %all-reduce.8.cloned.1.call-start = ((), (), s32[]{:S(2)}) async-start(), calls=%async_computation.2 | async-start | bytes 1048576 | tf_op jit(solution)/shard_map/psum | solution.py:75
  41.5 198.0 %all-to-all-start = ((bf16[16,2,6144]{2,1,0:T(2,128)(2,1)}), bf16[16,2,6144]{2,1,0:T(2,128)(2,1)S(1)}, u32[]{:S(2)}, u32[]{:S(2)}) async-start(bf16[16,2,6144]{2,1,0:T(2,128)(2,1)} %reshape.24), calls=%async_computation | async-start | bytes 786432 | tf_op jit(solution)/shard_map/all_to_all | solution.py:72
Sparse Core Ops, SparseCore 0:
  13.8 108.7 all-reduce.5
  128.3 109.3 all-reduce.7
where the time goes:
time: 419 us; the launch traced here: 415 us
  waiting for transfers between devices  187 us (45%)
  other arithmetic  104 us (25%)
  local copies, waits for them, and re-layouts  56.4 us (13%)
  blocking collectives  43 us (10%)
  between operations  14.1 us (3%)
  starting transfers between devices  8.26 us (2%)
    psum x2, waiting for transfers between devices, local(): lax.psum((s_y, s_ty, s_zero, s_one, s_two), 'date')  187 us
    convert_element_type x64, other arithmetic, step(): lax.dynamic_index_in_dim(piece, i, 0, keepdims=True).astype(jnp.float32)  45.1 us
    add x64, other arithmetic, step(): equal = equal + (other == own).astype(jnp.float32)  42.9 us
    all_gather x1, blocking collectives, local(): median = lax.all_gather(part_median, 'date', axis=1, tiled=True)  40.4 us
    unnamed x4, local copies, waits for them, and re-layouts  35 us
    all_to_all x1, local copies, waits for them, and re-layouts, local(): lax.all_to_all(marked, 'date', split_axis=2, concat_axis=0, tiled=True)  12.9 us
    convert_element_type x1, local copies, waits for them, and re-layouts, local(): jnp.where(valid[:, None, :] > 0, values, sentinel).astype(jnp.bfloat16)  8.54 us
  transfers between devices with their start and end apart: 3, of which 2 were waited for; matrix products, arithmetic and copies ran while one was open for 8% of the time, Pallas kernels for 0%

commit v1 on v0

v1 whole, which is shorter than its diff:
```python
import functools

import jax
import jax.numpy as jnp
from jax import lax
from jax.experimental import pallas as pl
from jax.experimental.pallas import tpu as pltpu
from jax.sharding import PartitionSpec as P

MESH = pl.DeviceIdType.MESH
ridge = 1.0
sentinel = 100.0
lanes = 128
slot = 8


def merge_pairs(lo, hi, r):
    step = r * 2
    if step < hi - lo:
        yield from merge_pairs(lo, hi, step)
        yield from merge_pairs(lo + r, hi, step)
        yield from ((i, i + r) for i in range(lo + r, hi - r, step))
    else:
        yield (lo, lo + r)


def sort_pairs(lo, hi):
    if hi - lo >= 1:
        mid = lo + (hi - lo) // 2
        yield from sort_pairs(lo, mid)
        yield from sort_pairs(mid + 1, hi)
        yield from merge_pairs(lo, hi, 1)


def sort_network(values):
    values = list(values)
    for i, j in sort_pairs(0, len(values) - 1):
        a, b = values[i], values[j]
        values[i], values[j] = jnp.minimum(a, b), jnp.maximum(a, b)
    return values


def kernel(
    n,
    pixes,
    x_ref,
    m_ref,
    days_ref,
    med_ref,
    slope_ref,
    wide,
    sent,
    got,
    part,
    parts,
    mean_row,
    mean_rows,
    mean_tile,
    year_tile,
    flip,
    data_send,
    data_recv,
    part_send,
    part_recv,
    mean_send,
    mean_recv,
    med_send,
    med_recv,
    slope_send,
    slope_recv,
):
    me = lax.axis_index("date")
    pix = lax.axis_index("pix")
    dates, bands, tile = x_ref.shape
    width = tile // n
    total = n * dates

    barrier = pltpu.get_barrier_semaphore()

    @pl.loop(1, n)
    def _(r):
        pl.semaphore_signal(barrier, inc=1, device_id={"date": lax.rem(me + r, n)}, device_id_type=MESH)

    for r in range(1, pixes):
        pl.semaphore_signal(barrier, inc=1, device_id={"pix": lax.rem(pix + r, pixes)}, device_id_type=MESH)

    def mark(j, carry):
        cols = pl.ds(pl.multiple_of(j * width, lanes), width)
        out = []
        for d in range(dates):
            x = x_ref[d, :, cols].astype(jnp.float32)
            valid = jnp.broadcast_to(m_ref[d : d + 1, cols], x.shape) > 0
            wide[d * bands : (d + 1) * bands, :] = jnp.where(valid, x, sentinel)
            csum, cnt = carry[d]
            csum = csum + jnp.where(valid, x, 0.0)
            cnt = cnt + jnp.where(valid, 1.0, 0.0)
            out.append((csum, cnt))
        sent[j] = wide[...].astype(jnp.bfloat16)
        return tuple(out)

    zero = jnp.zeros((bands, width), jnp.float32)
    sums = lax.fori_loop(0, n, mark, tuple((zero, zero) for _ in range(dates)))
    got[me] = sent[me]

    lane = lax.broadcasted_iota(jnp.int32, (bands, lanes), 1)
    band = lax.broadcasted_iota(jnp.int32, (bands, lanes), 0)
    lane_row = lax.broadcasted_iota(jnp.int32, (1, lanes), 1)
    row = jnp.zeros((bands, lanes), jnp.float32)
    count_row = jnp.zeros((bands, lanes), jnp.float32)
    for d in range(dates):
        csum = jnp.sum(sums[d][0], axis=1, keepdims=True)
        cnt = jnp.sum(sums[d][1], axis=1, keepdims=True)
        row = row + jnp.where(lane == d * slot + band, csum, 0.0)
        count_row = count_row + jnp.where((lane >= d * slot) & (lane < (d + 1) * slot) & (band == 0), cnt, 0.0)
    part[0:1, :] = jnp.sum(row, axis=0, keepdims=True)
    part[1:2, :] = jnp.sum(count_row, axis=0, keepdims=True)

    pl.semaphore_wait(barrier, n - 1 + pixes - 1)

    def part_copy(r):
        return pltpu.make_async_remote_copy(
            src_ref=part,
            dst_ref=parts.at[r],
            send_sem=part_send.at[r],
            recv_sem=part_recv.at[r],
            device_id={"pix": lax.rem(pix + r, pixes)},
            device_id_type=MESH,
        )

    for r in range(1, pixes):
        part_copy(r).start()

    def data_copy(r):
        j = lax.rem(me + r, n)
        return pltpu.make_async_remote_copy(
            src_ref=sent.at[j],
            dst_ref=got.at[me],
            send_sem=data_send.at[r],
            recv_sem=data_recv.at[r],
            device_id={"date": j},
            device_id_type=MESH,
        )

    @pl.loop(1, n)
    def _(r):
        data_copy(r).start()

    csum_row = part[0:1, :]
    cnt_row = part[1:2, :]
    for r in range(1, pixes):
        part_copy(r).wait_recv()
        csum_row = csum_row + parts[r, 0:1, :]
        cnt_row = cnt_row + parts[r, 1:2, :]
    means = csum_row / jnp.maximum(cnt_row, 1.0)
    for d in range(dates):
        year = jnp.full((1, lanes), days_ref[d], jnp.int32).astype(jnp.float32) / 365.0
        means = jnp.where(lane_row == d * slot + slot - 1, year, means)
    mean_row[...] = means
    mean_rows[me] = means

    def mean_copy(r):
        return pltpu.make_async_remote_copy(
            src_ref=mean_row,
            dst_ref=mean_rows.at[me],
            send_sem=mean_send.at[r],
            recv_sem=mean_recv.at[r],
            device_id={"date": lax.rem(me + r, n)},
            device_id_type=MESH,
        )

    @pl.loop(1, n)
    def _(r):
        mean_copy(r).start()

    @pl.loop(1, n)
    def _(r):
        mean_copy(r).wait_recv()

    @pl.loop(0, n)
    def _(j):
        line = jnp.broadcast_to(mean_rows[j], (bands, lanes))
        for d in range(dates):
            mean = jnp.sum(jnp.where(lane == d * slot + band, line, 0.0), axis=1, keepdims=True)
            year = jnp.sum(jnp.where(lane == d * slot + slot - 1, line, 0.0), axis=1, keepdims=True)
            mean_tile[j * dates + d] = jnp.broadcast_to(mean, (bands, lanes))
            year_tile[j * dates + d] = jnp.broadcast_to(year, (bands, lanes))

    @pl.loop(1, n)
    def _(r):
        data_copy(r).wait_recv()

    @pl.loop(0, width // lanes)
    def _(k):
        cols = pl.ds(pl.multiple_of(k * lanes, lanes), lanes)
        blank = jnp.zeros((bands, lanes), jnp.float32)

        def trend(j, carry):
            fill, s_zero, s_one, s_two, s_y, s_ty = carry
            block = got[j, :, cols].astype(jnp.float32)
            for d in range(dates):
                x = block[d * bands : (d + 1) * bands, :]
                year = year_tile[j * dates + d]
                valid = x < 50.0
                y = jnp.where(valid, x - mean_tile[j * dates + d], 0.0)
                m = jnp.where(valid, 1.0, 0.0)
                tm = year * m
                s_zero = s_zero + m
                s_one = s_one + tm
                s_two = s_two + year * tm
                s_y = s_y + y
                s_ty = s_ty + year * y
                flip[j * dates + d] = jnp.where(valid, x, fill)
                fill = jnp.where(valid, fill, -fill)
            return (fill, s_zero, s_one, s_two, s_y, s_ty)

        start = (blank + sentinel, blank, blank, blank, blank, blank)
        fill, s_zero, s_one, s_two, s_y, s_ty = lax.fori_loop(0, n, trend, start)
        first = s_zero + ridge
        slope = (first * s_ty - s_one * s_y) / (first * (s_two + ridge) - s_one * s_one)

        half = total // 2
        low = sort_network([flip[i] for i in range(half)])
        high = sort_network([flip[half + i] for i in range(half)])
        lower = None
        upper = None
        for i in range(half):
            a, b = low[i], high[half - 1 - i]
            small, large = jnp.minimum(a, b), jnp.maximum(a, b)
            lower = small if lower is None else jnp.maximum(lower, small)
            upper = large if upper is None else jnp.minimum(upper, large)
        median = jnp.where(fill < 0.0, lower, 0.5 * (lower + upper))
        here = pl.ds(pl.multiple_of(me * width + k * lanes, lanes), lanes)
        med_ref[:, here] = median
        slope_ref[:, here] = slope

    mine = pl.ds(pl.multiple_of(me * width, lanes), width)

    def out_copy(r, ref, send, recv):
        return pltpu.make_async_remote_copy(
            src_ref=ref.at[:, mine],
            dst_ref=ref.at[:, mine],
            send_sem=send.at[r],
            recv_sem=recv.at[r],
            device_id={"date": lax.rem(me + r, n)},
            device_id_type=MESH,
        )

    @pl.loop(1, n)
    def _(r):
        out_copy(r, med_ref, med_send, med_recv).start()
        out_copy(r, slope_ref, slope_send, slope_recv).start()

    for r in range(1, pixes):
        part_copy(r).wait_send()

    @pl.loop(1, n)
    def _(r):
        data_copy(r).wait_send()
        mean_copy(r).wait_send()

    @pl.loop(1, n)
    def _(r):
        out_copy(r, med_ref, med_send, med_recv).wait()
        out_copy(r, slope_ref, slope_send, slope_recv).wait()


def local(n, pixes, reflect, cloud_free, days):
    dates, bands, tile = reflect.shape
    width = tile // n
    out = jax.ShapeDtypeStruct((bands, tile), jnp.float32)
    vmem = pl.BlockSpec(memory_space=pltpu.VMEM)
    dma = pltpu.SemaphoreType.DMA
    return pl.pallas_call(
        functools.partial(kernel, n, pixes),
        out_shape=(out, out),
        in_specs=[vmem, vmem, pl.BlockSpec(memory_space=pltpu.SMEM)],
        out_specs=(vmem, vmem),
        scratch_shapes=[
            pltpu.VMEM((dates * bands, width), jnp.float32),
            pltpu.VMEM((n, dates * bands, width), jnp.bfloat16),
            pltpu.VMEM((n, dates * bands, width), jnp.bfloat16),
            pltpu.VMEM((2, lanes), jnp.float32),
            pltpu.VMEM((pixes, 2, lanes), jnp.float32),
            pltpu.VMEM((1, lanes), jnp.float32),
            pltpu.VMEM((n, 1, lanes), jnp.float32),
            pltpu.VMEM((n * dates, bands, lanes), jnp.float32),
            pltpu.VMEM((n * dates, bands, lanes), jnp.float32),
            pltpu.VMEM((n * dates, bands, lanes), jnp.float32),
            dma((n,)),
            dma((n,)),
            dma((pixes,)),
            dma((pixes,)),
            dma((n,)),
            dma((n,)),
            dma((n,)),
            dma((n,)),
            dma((n,)),
            dma((n,)),
        ],
        compiler_params=pltpu.CompilerParams(collective_id=0, has_side_effects=True),
    )(reflect, cloud_free, days)


def solution(mesh):
    placed = (P("date", None, "pix"), P("date", "pix"), P("date"))
    return jax.shard_map(
        functools.partial(local, mesh.shape["date"], mesh.shape["pix"]),
        mesh=mesh,
        in_specs=placed,
        out_specs=(P(None, "pix"), P(None, "pix")),
        check_vma=False,
    )
```

time: 419 us -> 38.8 us (0.09)
  the two profiles are of different devices: /device:TPU:0 before, /device:TPU:8 now
where the time goes in v1:
time: 38.8 us; the launch traced here: 38.6 us
  Pallas kernels  33.6 us (87%)
  local copies, waits for them, and re-layouts  4.42 us (11%)
  between operations  0.65 us (2%)
    pallas_call x1, Pallas kernels, local(): pl.pallas_call(functools.partial(kernel, n, pixes), out_shape=(out, out),...  33.6 us
    unnamed x5, local copies, waits for them, and re-layouts  4.42 us

profile of v1, /device:TPU:8, one launch (start us, length us, event | category | flops | bytes accessed | tf_op | source)
XLA Modules:
  0.0 38.6 jit_solution(16734953227155244629)
XLA Ops:
  0.6 2.0 %copy.5.x_ref = bf16[4,6,8192]{2,1,0:T(8,128)(2,1)} copy(bf16[4,6,8192]{2,0,1:T(4,128)(2,1)} %param.3) | data formatting | bytes 786432 | tf_op args[0]
  2.6 33.6 %shard_map.50 = (f32[6,8192]{1,0:T(8,128)}, f32[6,8192]{1,0:T(8,128)}) custom-call(bf16[4,6,8192]{2,1,0:T(8,128)(2,1)} %copy.5.x_ref, s32[4,8192]{1,0:T(4,128)} %m_ref.1, s32[4]{0:T(128)} %days_ref.1), custom_call_target="tpu_custom_call" | custom-call | tf_op jit(solution)/shard_map/pallas_call | solution.py:273
  36.2 0.0 copy-start
  36.2 1.7 %copy.8 = f32[6,8192]{1,0:T(8,128)} copy(f32[6,8192]{1,0:T(8,128)} %get-tuple-element.4) | data formatting | bytes 393216
  37.9 0.0 copy-done
  37.9 0.7 %copy.9 = f32[6,8192]{1,0:T(8,128)} copy(f32[6,8192]{1,0:T(8,128)S(1)} %copy-done) | data formatting | bytes 393216
Async XLA Ops:
  36.2 1.7 %copy-start = (f32[6,8192]{1,0:T(8,128)S(1)}, f32[6,8192]{1,0:T(8,128)}, u32[]{:S(2)}) copy-start(f32[6,8192]{1,0:T(8,128)} %get-tuple-element.5) | copy-start | bytes 589828

commit v2 on v1

v2 whole, which is shorter than its diff:
```python
import functools

import jax
import jax.numpy as jnp
from jax import lax
from jax.experimental import pallas as pl
from jax.experimental.pallas import tpu as pltpu
from jax.sharding import PartitionSpec as P

MESH = pl.DeviceIdType.MESH
ridge = 1.0
sentinel = 100.0
lanes = 128
slot = 8


def merge_pairs(lo, hi, r):
    step = r * 2
    if step < hi - lo:
        yield from merge_pairs(lo, hi, step)
        yield from merge_pairs(lo + r, hi, step)
        yield from ((i, i + r) for i in range(lo + r, hi - r, step))
    else:
        yield (lo, lo + r)


def sort_pairs(lo, hi):
    if hi - lo >= 1:
        mid = lo + (hi - lo) // 2
        yield from sort_pairs(lo, mid)
        yield from sort_pairs(mid + 1, hi)
        yield from merge_pairs(lo, hi, 1)


def sort_network(values):
    values = list(values)
    for i, j in sort_pairs(0, len(values) - 1):
        a, b = values[i], values[j]
        values[i], values[j] = jnp.minimum(a, b), jnp.maximum(a, b)
    return values


def kernel(
    n,
    pixes,
    group,
    x_hbm,
    m_hbm,
    days_ref,
    med_ref,
    slope_ref,
    x_ref,
    m_ref,
    wide,
    sent,
    got,
    part,
    parts,
    mean_row,
    mean_rows,
    stack,
    mean_tile,
    year_tile,
    flip,
    load_sem,
    data_send,
    data_recv,
    part_send,
    part_recv,
    mean_send,
    mean_recv,
    far_send,
    far_recv,
    near_send,
    near_recv,
):
    me = lax.axis_index("date")
    pix = lax.axis_index("pix")
    bands, dates, tile = x_ref.shape
    width = tile // n
    total = n * dates
    lines = n // group
    line = me // group
    spot = lax.rem(me, group)
    pieces = sent.shape[0]
    span = width // pieces

    barrier = pltpu.get_barrier_semaphore()

    @pl.loop(1, n)
    def _(r):
        pl.semaphore_signal(barrier, inc=1, device_id={"date": lax.rem(me + r, n)}, device_id_type=MESH)

    for r in range(1, pixes):
        pl.semaphore_signal(barrier, inc=1, device_id={"pix": lax.rem(pix + r, pixes)}, device_id_type=MESH)

    load_x = pltpu.make_async_copy(x_hbm, x_ref, load_sem.at[0])
    load_m = pltpu.make_async_copy(m_hbm, m_ref, load_sem.at[1])
    load_x.start()
    load_m.start()
    stack[...] = jnp.zeros_like(stack)
    load_m.wait()
    load_x.wait()

    def mark(j, carry):
        cols = pl.ds(pl.multiple_of(j * width, lanes), width)
        valid = m_ref[:, cols] > 0
        out = []
        for b in range(bands):
            x = x_ref[b, :, cols].astype(jnp.float32)
            marked = jnp.where(valid, x, sentinel)
            for d in range(dates):
                wide[d * bands + b : d * bands + b + 1, :] = marked[d : d + 1, :]
            out.append(carry[b] + jnp.where(valid, x, 0.0))
        for p in range(pieces):
            sent[p, j] = wide[:, p * span : (p + 1) * span].astype(jnp.bfloat16)
        out.append(carry[bands] + jnp.where(valid, 1.0, 0.0))
        return tuple(out)

    zero = jnp.zeros((dates, width), jnp.float32)
    sums = lax.fori_loop(0, n, mark, tuple(zero for _ in range(bands + 1)))
    for p in range(pieces):
        got[p, me] = sent[p, me]

    lane = lax.broadcasted_iota(jnp.int32, (dates, lanes), 1)
    date = lax.broadcasted_iota(jnp.int32, (dates, lanes), 0)
    lane_row = lax.broadcasted_iota(jnp.int32, (1, lanes), 1)
    row = jnp.zeros((dates, lanes), jnp.float32)
    for b in range(bands):
        row = row + jnp.where(lane == date * slot + b, jnp.sum(sums[b], axis=1, keepdims=True), 0.0)
    own = (lane >= date * slot) & (lane < (date + 1) * slot)
    count_row = jnp.where(own, jnp.sum(sums[bands], axis=1, keepdims=True), 0.0)
    part[0:1, :] = jnp.sum(row, axis=0, keepdims=True)
    part[1:2, :] = jnp.sum(count_row, axis=0, keepdims=True)

    pl.semaphore_wait(barrier, n - 1 + pixes - 1)

    def part_copy(r):
        return pltpu.make_async_remote_copy(
            src_ref=part,
            dst_ref=parts.at[r],
            send_sem=part_send.at[r],
            recv_sem=part_recv.at[r],
            device_id={"pix": lax.rem(pix + r, pixes)},
            device_id_type=MESH,
        )

    for r in range(1, pixes):
        part_copy(r).start()

    def data_copy(p, r):
        j = lax.rem(me + r, n)
        return pltpu.make_async_remote_copy(
            src_ref=sent.at[p, j],
            dst_ref=got.at[p, me],
            send_sem=data_send.at[p, r],
            recv_sem=data_recv.at[p, r],
            device_id={"date": j},
            device_id_type=MESH,
        )

    def mean_copy(r):
        return pltpu.make_async_remote_copy(
            src_ref=mean_row,
            dst_ref=mean_rows.at[me],
            send_sem=mean_send.at[r],
            recv_sem=mean_recv.at[r],
            device_id={"date": lax.rem(me + r, n)},
            device_id_type=MESH,
        )

    @pl.loop(1, n)
    def _(r):
        data_copy(0, r).start()

    csum_row = part[0:1, :]
    cnt_row = part[1:2, :]
    for r in range(1, pixes):
        part_copy(r).wait_recv()
        csum_row = csum_row + parts[r, 0:1, :]
        cnt_row = cnt_row + parts[r, 1:2, :]
    means = csum_row / jnp.maximum(cnt_row, 1.0)
    years = jnp.zeros((1, lanes), jnp.float32)
    for d in range(dates):
        year = jnp.full((1, lanes), days_ref[d], jnp.int32).astype(jnp.float32) / 365.0
        years = jnp.where((lane_row >= d * slot) & (lane_row < (d + 1) * slot), year, years)
    mean_row[0:1, :] = means
    mean_row[1:2, :] = years
    mean_rows[me] = mean_row[...]

    @pl.loop(1, n)
    def _(r):
        mean_copy(r).start()

    for p in range(1, pieces):

        @pl.loop(1, n)
        def _(r):
            data_copy(p, r).start()

    @pl.loop(1, n)
    def _(r):
        mean_copy(r).wait_recv()

    for row_index, out_ref in ((0, mean_tile), (1, year_tile)):
        for j in range(n):
            stack[j : j + 1, :] = mean_rows[j, row_index : row_index + 1, :]
        turned = jnp.transpose(stack[...])
        for j in range(n):
            for d in range(dates):
                column = turned[d * slot : d * slot + bands, j : j + 1]
                out_ref[j * dates + d] = jnp.broadcast_to(column, (bands, lanes))

    def rank(p, k):
        cols = pl.ds(pl.multiple_of(k * lanes, lanes), lanes)
        blank = jnp.zeros((bands, lanes), jnp.float32)

        def trend(j, carry):
            fill, s_zero, s_one, s_two, s_y, s_ty = carry
            block = got[p, j, :, cols].astype(jnp.float32)
            for d in range(dates):
                x = block[d * bands : (d + 1) * bands, :]
                year = year_tile[j * dates + d]
                valid = x < 50.0
                y = jnp.where(valid, x - mean_tile[j * dates + d], 0.0)
                m = jnp.where(valid, 1.0, 0.0)
                tm = year * m
                s_zero = s_zero + m
                s_one = s_one + tm
                s_two = s_two + year * tm
                s_y = s_y + y
                s_ty = s_ty + year * y
                flip[j * dates + d] = jnp.where(valid, x, fill)
                fill = jnp.where(valid, fill, -fill)
            return (fill, s_zero, s_one, s_two, s_y, s_ty)

        start = (blank + sentinel, blank, blank, blank, blank, blank)
        fill, s_zero, s_one, s_two, s_y, s_ty = lax.fori_loop(0, n, trend, start)
        first = s_zero + ridge
        slope = (first * s_ty - s_one * s_y) / (first * (s_two + ridge) - s_one * s_one)

        half = total // 2
        low = sort_network([flip[i] for i in range(half)])
        high = sort_network([flip[half + i] for i in range(half)])
        lower = None
        upper = None
        for i in range(half):
            a, b = low[i], high[half - 1 - i]
            small, large = jnp.minimum(a, b), jnp.maximum(a, b)
            lower = small if lower is None else jnp.maximum(lower, small)
            upper = large if upper is None else jnp.minimum(upper, large)
        median = jnp.where(fill < 0.0, lower, 0.5 * (lower + upper))
        here = pl.ds(pl.multiple_of(me * width + p * span + k * lanes, lanes), lanes)
        med_ref[:, here] = median
        slope_ref[:, here] = slope

    refs = (med_ref, slope_ref)

    def out_copy(ref, owner, p, target, send, recv):
        cols = pl.ds(pl.multiple_of(owner * width + p * span, lanes), span)
        return pltpu.make_async_remote_copy(
            src_ref=ref.at[:, cols],
            dst_ref=ref.at[:, cols],
            send_sem=send,
            recv_sem=recv,
            device_id={"date": target},
            device_id_type=MESH,
        )

    def far_copies(p, r):
        target = lax.rem(line + r, lines) * group + spot
        return [out_copy(refs[i], me, p, target, far_send.at[p, r, i], far_recv.at[p, r, i]) for i in range(2)]

    def near_copies(p, r, s):
        owner = lax.rem(line + lines - r, lines) * group + spot
        target = line * group + lax.rem(spot + s, group)
        return [
            out_copy(refs[i], owner, p, target, near_send.at[p, r, s, i], near_recv.at[p, r, s, i]) for i in range(2)
        ]

    for p in range(pieces):

        @pl.loop(1, n)
        def _(r):
            data_copy(p, r).wait_recv()

        @pl.loop(0, span // lanes)
        def _(k):
            rank(p, k)

        for r in range(1, lines):
            for copy in far_copies(p, r):
                copy.start()
        for s in range(1, group):
            for copy in near_copies(p, 0, s):
                copy.start()

    for p in range(pieces):
        for r in range(1, lines):
            for copy in far_copies(p, r):
                copy.wait_recv()
            for s in range(1, group):
                for copy in near_copies(p, r, s):
                    copy.start()

    for r in range(1, pixes):
        part_copy(r).wait_send()

    @pl.loop(1, n)
    def _(r):
        mean_copy(r).wait_send()
        for p in range(pieces):
            data_copy(p, r).wait_send()

    for p in range(pieces):
        for r in range(1, lines):
            for copy in far_copies(p, r):
                copy.wait_send()
        for r in range(lines):
            for s in range(1, group):
                for copy in near_copies(p, r, s):
                    copy.wait()


def local(n, pixes, reflect, cloud_free, days):
    dates, bands, tile = reflect.shape
    width = tile // n
    group = 1
    while group * group * 4 <= n and n % (group * 2) == 0:
        group *= 2
    pieces = 2 if width % (2 * lanes) == 0 else 1
    span = width // pieces
    lines = n // group
    turned = -(-n // lanes) * lanes
    out = jax.ShapeDtypeStruct((bands, tile), jnp.float32)
    vmem = pl.BlockSpec(memory_space=pltpu.VMEM)
    hbm = pl.BlockSpec(memory_space=pl.ANY)
    dma = pltpu.SemaphoreType.DMA
    return pl.pallas_call(
        functools.partial(kernel, n, pixes, group),
        out_shape=(out, out),
        in_specs=[hbm, hbm, pl.BlockSpec(memory_space=pltpu.SMEM)],
        out_specs=(vmem, vmem),
        scratch_shapes=[
            pltpu.VMEM((bands, dates, tile), jnp.bfloat16),
            pltpu.VMEM((dates, tile), jnp.int32),
            pltpu.VMEM((dates * bands, width), jnp.float32),
            pltpu.VMEM((pieces, n, dates * bands, span), jnp.bfloat16),
            pltpu.VMEM((pieces, n, dates * bands, span), jnp.bfloat16),
            pltpu.VMEM((2, lanes), jnp.float32),
            pltpu.VMEM((pixes, 2, lanes), jnp.float32),
            pltpu.VMEM((2, lanes), jnp.float32),
            pltpu.VMEM((n, 2, lanes), jnp.float32),
            pltpu.VMEM((turned, lanes), jnp.float32),
            pltpu.VMEM((n * dates, bands, lanes), jnp.float32),
            pltpu.VMEM((n * dates, bands, lanes), jnp.float32),
            pltpu.VMEM((n * dates, bands, lanes), jnp.float32),
            dma((2,)),
            dma((pieces, n)),
            dma((pieces, n)),
            dma((pixes,)),
            dma((pixes,)),
            dma((n,)),
            dma((n,)),
            dma((pieces, lines, 2)),
            dma((pieces, lines, 2)),
            dma((pieces, lines, group, 2)),
            dma((pieces, lines, group, 2)),
        ],
        compiler_params=pltpu.CompilerParams(collective_id=0, has_side_effects=True),
    )(jnp.transpose(reflect, (1, 0, 2)), cloud_free, days)


def solution(mesh):
    placed = (P("date", None, "pix"), P("date", "pix"), P("date"))
    return jax.shard_map(
        functools.partial(local, mesh.shape["date"], mesh.shape["pix"]),
        mesh=mesh,
        in_specs=placed,
        out_specs=(P(None, "pix"), P(None, "pix")),
        check_vma=False,
    )
```

time: 38.8 us -> 33.7 us (0.87)
  the two profiles are of different devices: /device:TPU:8 before, /device:TPU:0 now
where the time goes in v2:
time: 33.7 us; the launch traced here: 33.6 us
  Pallas kernels  30.5 us (91%)
  local copies, waits for them, and re-layouts  2.42 us (7%)
  between operations  0.65 us (2%)
    pallas_call x1, Pallas kernels, local(): pl.pallas_call(functools.partial(kernel, n, pixes, group), out_shape=(out...  30.5 us
    unnamed x4, local copies, waits for them, and re-layouts  2.42 us

profile of v2, /device:TPU:0, one launch (start us, length us, event | category | flops | bytes accessed | tf_op | source)
XLA Modules:
  0.0 33.6 jit_solution(9012915468825988080)
XLA Ops:
  0.6 30.5 %shard_map.50 = (f32[6,8192]{1,0:T(8,128)}, f32[6,8192]{1,0:T(8,128)}) custom-call(bf16[6,4,8192]{2,1,0:T(4,128)(2,1)} %bitcast.1, s32[4,8192]{1,0:T(4,128)} %m_hbm.1, s32[4]{0:T(128)} %days_ref.1), custom_call_target="tpu_custom_call" | custom-call | tf_op jit(solution)/shard_map/pallas_call | solution.py:339
  31.1 0.0 copy-start
  31.2 1.7 %copy.7 = f32[6,8192]{1,0:T(8,128)} copy(f32[6,8192]{1,0:T(8,128)} %get-tuple-element.4) | data formatting | bytes 393216
  32.9 0.0 copy-done
  32.9 0.7 %copy.8 = f32[6,8192]{1,0:T(8,128)} copy(f32[6,8192]{1,0:T(8,128)S(1)} %copy-done) | data formatting | bytes 393216
Async XLA Ops:
  31.1 1.7 %copy-start = (f32[6,8192]{1,0:T(8,128)S(1)}, f32[6,8192]{1,0:T(8,128)}, u32[]{:S(2)}) copy-start(f32[6,8192]{1,0:T(8,128)} %get-tuple-element.5) | copy-start | bytes 589828

commit v3 on v2

--- a/solution.py
+++ b/solution.py
@@ -47,8 +47,7 @@
     x_hbm,
     m_hbm,
     days_ref,
-    med_ref,
-    slope_ref,
+    out_ref,
     x_ref,
     m_ref,
     wide,
@@ -202,14 +201,14 @@
     def _(r):
         mean_copy(r).wait_recv()
 
-    for row_index, out_ref in ((0, mean_tile), (1, year_tile)):
+    for row_index, tile_ref in ((0, mean_tile), (1, year_tile)):
         for j in range(n):
             stack[j : j + 1, :] = mean_rows[j, row_index : row_index + 1, :]
         turned = jnp.transpose(stack[...])
         for j in range(n):
             for d in range(dates):
                 column = turned[d * slot : d * slot + bands, j : j + 1]
-                out_ref[j * dates + d] = jnp.broadcast_to(column, (bands, lanes))
+                tile_ref[j * dates + d] = jnp.broadcast_to(column, (bands, lanes))
 
     def rank(p, k):
         cols = pl.ds(pl.multiple_of(k * lanes, lanes), lanes)
@@ -251,32 +250,28 @@
             upper = large if upper is None else jnp.minimum(upper, large)
         median = jnp.where(fill < 0.0, lower, 0.5 * (lower + upper))
         here = pl.ds(pl.multiple_of(me * width + p * span + k * lanes, lanes), lanes)
-        med_ref[:, here] = median
-        slope_ref[:, here] = slope
-
-    refs = (med_ref, slope_ref)
-
-    def out_copy(ref, owner, p, target, send, recv):
+        out_ref[0, :, here] = median
+        out_ref[1, :, here] = slope
+
+    def out_copy(owner, p, target, send, recv):
         cols = pl.ds(pl.multiple_of(owner * width + p * span, lanes), span)
         return pltpu.make_async_remote_copy(
-            src_ref=ref.at[:, cols],
-            dst_ref=ref.at[:, cols],
+            src_ref=out_ref.at[:, :, cols],
+            dst_ref=out_ref.at[:, :, cols],
             send_sem=send,
             recv_sem=recv,
             device_id={"date": target},
             device_id_type=MESH,
         )
 
-    def far_copies(p, r):
+    def far_copy(p, r):
         target = lax.rem(line + r, lines) * group + spot
-        return [out_copy(refs[i], me, p, target, far_send.at[p, r, i], far_recv.at[p, r, i]) for i in range(2)]
-
-    def near_copies(p, r, s):
+        return out_copy(me, p, target, far_send.at[p, r], far_recv.at[p, r])
+
+    def near_copy(p, r, s):
         owner = lax.rem(line + lines - r, lines) * group + spot
         target = line * group + lax.rem(spot + s, group)
-        return [
-            out_copy(refs[i], owner, p, target, near_send.at[p, r, s, i], near_recv.at[p, r, s, i]) for i in range(2)
-        ]
+        return out_copy(owner, p, target, near_send.at[p, r, s], near_recv.at[p, r, s])
 
     for p in range(pieces):
 
@@ -289,19 +284,15 @@
             rank(p, k)
 
         for r in range(1, lines):
-            for copy in far_copies(p, r):
-                copy.start()
+            far_copy(p, r).start()
         for s in range(1, group):
-            for copy in near_copies(p, 0, s):
-                copy.start()
+            near_copy(p, 0, s).start()
 
     for p in range(pieces):
         for r in range(1, lines):
-            for copy in far_copies(p, r):
-                copy.wait_recv()
+            far_copy(p, r).wait_recv()
             for s in range(1, group):
-                for copy in near_copies(p, r, s):
-                    copy.start()
+                near_copy(p, r, s).start()
 
     for r in range(1, pixes):
         part_copy(r).wait_send()
@@ -314,12 +305,10 @@
 
     for p in range(pieces):
         for r in range(1, lines):
-            for copy in far_copies(p, r):
-                copy.wait_send()
+            far_copy(p, r).wait_send()
         for r in range(lines):
             for s in range(1, group):
-                for copy in near_copies(p, r, s):
-                    copy.wait()
+                near_copy(p, r, s).wait()
 
 
 def local(n, pixes, reflect, cloud_free, days):
@@ -332,15 +321,14 @@
     span = width // pieces
     lines = n // group
     turned = -(-n // lanes) * lanes
-    out = jax.ShapeDtypeStruct((bands, tile), jnp.float32)
     vmem = pl.BlockSpec(memory_space=pltpu.VMEM)
     hbm = pl.BlockSpec(memory_space=pl.ANY)
     dma = pltpu.SemaphoreType.DMA
-    return pl.pallas_call(
+    out = pl.pallas_call(
         functools.partial(kernel, n, pixes, group),
-        out_shape=(out, out),
+        out_shape=pltpu.VMEM((2, bands, tile), jnp.float32),
         in_specs=[hbm, hbm, pl.BlockSpec(memory_space=pltpu.SMEM)],
-        out_specs=(vmem, vmem),
+        out_specs=vmem,
         scratch_shapes=[
             pltpu.VMEM((bands, dates, tile), jnp.bfloat16),
             pltpu.VMEM((dates, tile), jnp.int32),
@@ -362,13 +350,14 @@
             dma((pixes,)),
             dma((n,)),
             dma((n,)),
-            dma((pieces, lines, 2)),
-            dma((pieces, lines, 2)),
-            dma((pieces, lines, group, 2)),
-            dma((pieces, lines, group, 2)),
+            dma((pieces, lines)),
+            dma((pieces, lines)),
+            dma((pieces, lines, group)),
+            dma((pieces, lines, group)),
         ],
         compiler_params=pltpu.CompilerParams(collective_id=0, has_side_effects=True),
     )(jnp.transpose(reflect, (1, 0, 2)), cloud_free, days)
+    return (out[0], out[1])
 
 
 def solution(mesh):

time: 33.7 us -> 30.6 us (0.908)
  local copies, waits for them, and re-layouts: 2.42 us -> 0.82 us
  Pallas kernels: 30.5 us -> 29 us
    unnamed x4 -> x0, local copies, waits for them, and re-layouts: 2.42 us -> none
    pallas_call x1, Pallas kernels: 30.5 us -> 29 us  [local(): pl.pallas_call(functools.partial(kernel, n, pixes, group), out_shape=pltp...]
    squeeze x0 -> x1, local copies, waits for them, and re-layouts: none -> 0.82 us  [local(): return (out[0], out[1])]
where the time goes in v3:
time: 30.6 us; the launch traced here: 30.4 us
  Pallas kernels  29 us (95%)
  local copies, waits for them, and re-layouts  0.82 us (3%)
  between operations  0.64 us (2%)
    pallas_call x1, Pallas kernels, local(): pl.pallas_call(functools.partial(kernel, n, pixes, group), out_shape=pltp...  29 us
    squeeze x1, local copies, waits for them, and re-layouts, local(): return (out[0], out[1])  0.82 us

profile of v3, /device:TPU:0, one launch (start us, length us, event | category | flops | bytes accessed | tf_op | source)
XLA Modules:
  0.0 30.4 jit_solution(9784061882372192487)
XLA Ops:
  0.6 29.0 %shard_map.50 = f32[2,6,8192]{2,1,0:T(8,128)S(1)} custom-call(bf16[6,4,8192]{2,1,0:T(4,128)(2,1)} %bitcast.5, s32[4,8192]{1,0:T(4,128)} %m_hbm.1, s32[4]{0:T(128)} %days_ref.1), custom_call_target="tpu_custom_call" | custom-call | tf_op jit(solution)/shard_map/pallas_call | solution.py:327
  29.6 0.8 %slice_bitcast_fusion = (f32[6,8192]{1,0:T(8,128)}, f32[6,8192]{1,0:T(8,128)}) fusion(f32[2,6,8192]{2,1,0:T(8,128)S(1)} %shard_map.50), kind=kLoop, calls=%fused_computation | loop fusion | bytes 786432 | tf_op jit(solution)/shard_map/squeeze | solution.py:360

commit v4 on v3

--- a/solution.py
+++ b/solution.py
@@ -61,6 +61,7 @@
     mean_tile,
     year_tile,
     flip,
+    odd,
     load_sem,
     data_send,
     data_recv,
@@ -210,48 +211,57 @@
                 column = turned[d * slot : d * slot + bands, j : j + 1]
                 tile_ref[j * dates + d] = jnp.broadcast_to(column, (bands, lanes))
 
-    def rank(p, k):
-        cols = pl.ds(pl.multiple_of(k * lanes, lanes), lanes)
-        blank = jnp.zeros((bands, lanes), jnp.float32)
-
-        def trend(j, carry):
-            fill, s_zero, s_one, s_two, s_y, s_ty = carry
-            block = got[p, j, :, cols].astype(jnp.float32)
-            for d in range(dates):
-                x = block[d * bands : (d + 1) * bands, :]
-                year = year_tile[j * dates + d]
-                valid = x < 50.0
-                y = jnp.where(valid, x - mean_tile[j * dates + d], 0.0)
-                m = jnp.where(valid, 1.0, 0.0)
-                tm = year * m
-                s_zero = s_zero + m
-                s_one = s_one + tm
-                s_two = s_two + year * tm
-                s_y = s_y + y
-                s_ty = s_ty + year * y
-                flip[j * dates + d] = jnp.where(valid, x, fill)
-                fill = jnp.where(valid, fill, -fill)
-            return (fill, s_zero, s_one, s_two, s_y, s_ty)
-
-        start = (blank + sentinel, blank, blank, blank, blank, blank)
-        fill, s_zero, s_one, s_two, s_y, s_ty = lax.fori_loop(0, n, trend, start)
+    def trend(p, r, carry):
+        j = lax.rem(me + n - r, n)
+        fill, s_zero, s_one, s_two, s_y, s_ty = carry
+        block = got[p, j].astype(jnp.float32)
+        for d in range(dates):
+            x = block[d * bands : (d + 1) * bands, :]
+            year = jnp.concatenate([year_tile[j * dates + d]] * (span // lanes), axis=1)
+            mean = jnp.concatenate([mean_tile[j * dates + d]] * (span // lanes), axis=1)
+            valid = x < 50.0
+            y = jnp.where(valid, x - mean, 0.0)
+            m = jnp.where(valid, 1.0, 0.0)
+            tm = year * m
+            s_zero = s_zero + m
+            s_one = s_one + tm
+            s_two = s_two + year * tm
+            s_y = s_y + y
+            s_ty = s_ty + year * y
+            flip[r * dates + d] = jnp.where(valid, x, fill)
+            fill = jnp.where(valid, fill, -fill)
+        return (fill, s_zero, s_one, s_two, s_y, s_ty)
+
+    def rank(p):
+        blank = jnp.zeros((bands, span), jnp.float32)
+        start = trend(p, 0, (blank + sentinel, blank, blank, blank, blank, blank))
+
+        def arrived(r, carry):
+            data_copy(p, r).wait_recv()
+            return trend(p, r, carry)
+
+        fill, s_zero, s_one, s_two, s_y, s_ty = lax.fori_loop(1, n, arrived, start)
         first = s_zero + ridge
-        slope = (first * s_ty - s_one * s_y) / (first * (s_two + ridge) - s_one * s_one)
-
-        half = total // 2
-        low = sort_network([flip[i] for i in range(half)])
-        high = sort_network([flip[half + i] for i in range(half)])
-        lower = None
-        upper = None
-        for i in range(half):
-            a, b = low[i], high[half - 1 - i]
-            small, large = jnp.minimum(a, b), jnp.maximum(a, b)
-            lower = small if lower is None else jnp.maximum(lower, small)
-            upper = large if upper is None else jnp.minimum(upper, large)
-        median = jnp.where(fill < 0.0, lower, 0.5 * (lower + upper))
-        here = pl.ds(pl.multiple_of(me * width + p * span + k * lanes, lanes), lanes)
-        out_ref[0, :, here] = median
-        out_ref[1, :, here] = slope
+        here = pl.ds(pl.multiple_of(me * width + p * span, lanes), span)
+        out_ref[1, :, here] = (first * s_ty - s_one * s_y) / (first * (s_two + ridge) - s_one * s_one)
+        odd[...] = jnp.where(fill < 0.0, 1.0, 0.0)
+
+        @pl.loop(0, span // lanes)
+        def _(k):
+            cols = pl.ds(pl.multiple_of(k * lanes, lanes), lanes)
+            half = total // 2
+            low = sort_network([flip[i, :, cols] for i in range(half)])
+            high = sort_network([flip[half + i, :, cols] for i in range(half)])
+            lower = None
+            upper = None
+            for i in range(half):
+                a, b = low[i], high[half - 1 - i]
+                small, large = jnp.minimum(a, b), jnp.maximum(a, b)
+                lower = small if lower is None else jnp.maximum(lower, small)
+                upper = large if upper is None else jnp.minimum(upper, large)
+            median = jnp.where(odd[:, cols] > 0.5, lower, 0.5 * (lower + upper))
+            there = pl.ds(pl.multiple_of(me * width + p * span + k * lanes, lanes), lanes)
+            out_ref[0, :, there] = median
 
     def out_copy(owner, p, target, send, recv):
         cols = pl.ds(pl.multiple_of(owner * width + p * span, lanes), span)
@@ -264,26 +274,26 @@
             device_id_type=MESH,
         )
 
+    def partner(r):
+        other = line
+        for bit in range(lines.bit_length() - 1):
+            if (r >> bit) & 1:
+                other = other + (1 << bit) - (1 << (bit + 1)) * lax.rem(line // (1 << bit), 2)
+        return other
+
     def far_copy(p, r):
-        target = lax.rem(line + r, lines) * group + spot
+        target = partner(r) * group + spot
         return out_copy(me, p, target, far_send.at[p, r], far_recv.at[p, r])
 
     def near_copy(p, r, s):
-        owner = lax.rem(line + lines - r, lines) * group + spot
+        owner = partner(r) * group + spot
         target = line * group + lax.rem(spot + s, group)
         return out_copy(owner, p, target, near_send.at[p, r, s], near_recv.at[p, r, s])
 
     for p in range(pieces):
-
-        @pl.loop(1, n)
-        def _(r):
-            data_copy(p, r).wait_recv()
-
-        @pl.loop(0, span // lanes)
-        def _(k):
-            rank(p, k)
-
-        for r in range(1, lines):
+        rank(p)
+
+        for r in range(lines - 1, 0, -1):
             far_copy(p, r).start()
         for s in range(1, group):
             near_copy(p, 0, s).start()
@@ -342,7 +352,8 @@
             pltpu.VMEM((turned, lanes), jnp.float32),
             pltpu.VMEM((n * dates, bands, lanes), jnp.float32),
             pltpu.VMEM((n * dates, bands, lanes), jnp.float32),
-            pltpu.VMEM((n * dates, bands, lanes), jnp.float32),
+            pltpu.VMEM((n * dates, bands, span), jnp.float32),
+            pltpu.VMEM((bands, span), jnp.float32),
             dma((2,)),
             dma((pieces, n)),
             dma((pieces, n)),

time: 30.6 us -> 29.8 us (0.974)
  Pallas kernels: 29 us -> 28.2 us
    pallas_call x1, Pallas kernels: 29 us -> 28.2 us  [local(): pl.pallas_call(functools.partial(kernel, n, pixes, group), out_shape=pltp...]
where the time goes in v4:
time: 29.8 us; the launch traced here: 29.6 us
  Pallas kernels  28.2 us (95%)
  local copies, waits for them, and re-layouts  0.82 us (3%)
  between operations  0.64 us (2%)
    pallas_call x1, Pallas kernels, local(): pl.pallas_call(functools.partial(kernel, n, pixes, group), out_shape=pltp...  28.2 us
    squeeze x1, local copies, waits for them, and re-layouts, local(): return (out[0], out[1])  0.82 us

profile of v4, /device:TPU:0, one launch (start us, length us, event | category | flops | bytes accessed | tf_op | source)
XLA Modules:
  0.0 29.6 jit_solution(14943659009709617152)
XLA Ops:
  0.6 28.2 %shard_map.50 = f32[2,6,8192]{2,1,0:T(8,128)S(1)} custom-call(bf16[6,4,8192]{2,1,0:T(4,128)(2,1)} %bitcast.5, s32[4,8192]{1,0:T(4,128)} %m_hbm.1, s32[4]{0:T(128)} %days_ref.1), custom_call_target="tpu_custom_call" | custom-call | tf_op jit(solution)/shard_map/pallas_call | solution.py:337
  28.8 0.8 %slice_bitcast_fusion = (f32[6,8192]{1,0:T(8,128)}, f32[6,8192]{1,0:T(8,128)}) fusion(f32[2,6,8192]{2,1,0:T(8,128)S(1)} %shard_map.50), kind=kLoop, calls=%fused_computation | loop fusion | bytes 786432 | tf_op jit(solution)/shard_map/squeeze | solution.py:371
